TPU v7x, 32 devices: a whole 2x2x4 slice. The times are simulated.
32 devices in a mesh: sub: 8 (over z, core), sta: 4 (over y, x).
Axes of the slice: x: 2, y: 2, z: 4, core: 2. Of those that a mesh axis runs over, the one named last changes fastest.
Arguments:
- voltages: bfloat16 [8, 2, 64, 65536], P('sub', None, 'sta'), may hold values from -6 to 6
- beam_weights: bfloat16 [8, 2, 32, 64], P('sub'), may hold values from -0.5 to 0.5
- station_delays: int32 [64], P('sta'), may hold values from 0 to 16383
- dm_index: int32 [32, 1], P('sta'), may hold values from 1 to 8
Outputs:
- dedispersed: float32 [8, 2, 32, 1, 65536], P(None, None, None, None, ('sub', 'sta'))
- intensity: float32 [32, 1, 65536], P(None, None, ('sub', 'sta'))
Inputs may be any that keep to these rules, and one draw needn't show every extreme that they name: `station_delays`: delays in whole samples. `dm_index`: dispersion measure in steps of 10.
All inputs are finite; a program needn't handle non-finite values.
Results may differ from a plain program's by a relative error of at most 0.0006.
Values may be sent and summed in bfloat16 or wider, within the bound.
A program may use at most 320 MiB of HBM per device.

v0:
```python
import jax
import jax.numpy as jnp
from jax import lax
from jax.sharding import PartitionSpec as P

ROOT = 256
TWO_PI = 6.283185307179586
DISPERSION = 4148808000.0
DM_STEP = 10.0
BASE_FREQ = 120.0
CHANNEL_WIDTH = 0.1953125
HIGHEST = lax.Precision.HIGHEST


def angle_tables(rows_len, modulus):
    first = jnp.arange(rows_len, dtype=jnp.int32)[:, None]
    second = jnp.arange(rows_len, dtype=jnp.int32)[None, :]
    product = first * second % modulus
    angles = TWO_PI * product.astype(jnp.float32) / modulus
    return (jnp.cos(angles), jnp.sin(angles))


def chirp_base(subband, root_len, total_len):
    first = jnp.arange(root_len, dtype=jnp.int32)[:, None]
    second = jnp.arange(root_len, dtype=jnp.int32)[None, :]
    positions = first + root_len * second
    signed_bin = jnp.where(positions < total_len // 2, positions, positions - total_len)
    offset = (CHANNEL_WIDTH * signed_bin.astype(jnp.float32) / total_len)[None]
    centre = (BASE_FREQ + CHANNEL_WIDTH * (subband.astype(jnp.float32) + 0.5))[:, None, None]
    return TWO_PI * DISPERSION * offset * offset / (centre * centre * (centre + offset))


def left_dft(cos_table, sin_table, x_real, x_imag, flip_sign):
    real_part = jnp.einsum(
        "kt,...tu->...ku", cos_table, x_real, precision=HIGHEST
    ) + flip_sign * jnp.einsum("kt,...tu->...ku", sin_table, x_imag, precision=HIGHEST)
    imag_part = jnp.einsum(
        "kt,...tu->...ku", cos_table, x_imag, precision=HIGHEST
    ) - flip_sign * jnp.einsum("kt,...tu->...ku", sin_table, x_real, precision=HIGHEST)
    return (real_part, imag_part)


def right_dft(cos_table, sin_table, x_real, x_imag, flip_sign):
    real_part = jnp.einsum(
        "...kt,tm->...km", x_real, cos_table, precision=HIGHEST
    ) + flip_sign * jnp.einsum("...kt,tm->...km", x_imag, sin_table, precision=HIGHEST)
    imag_part = jnp.einsum(
        "...kt,tm->...km", x_imag, cos_table, precision=HIGHEST
    ) - flip_sign * jnp.einsum("...kt,tm->...km", x_real, sin_table, precision=HIGHEST)
    return (real_part, imag_part)


def beam_terms(w_block, v_real, v_imag):
    w_real = w_block[:, 0]
    w_imag = w_block[:, 1]
    real_part = jnp.einsum(
        "sbk,skt->bst", w_real, v_real, preferred_element_type=jnp.float32
    ) - jnp.einsum("sbk,skt->bst", w_imag, v_imag, preferred_element_type=jnp.float32)
    imag_part = jnp.einsum(
        "sbk,skt->bst", w_real, v_imag, preferred_element_type=jnp.float32
    ) + jnp.einsum("sbk,skt->bst", w_imag, v_real, preferred_element_type=jnp.float32)
    return jnp.stack([real_part, imag_part], axis=2)


def shards(voltages, beam_weights, station_delays, dm_index):
    sub_dev = voltages.shape[0]
    total_len = voltages.shape[3]
    local_beams = dm_index.shape[0]
    trials = dm_index.shape[1]
    root_len = ROOT
    doubled = jnp.concatenate([voltages, voltages], axis=3)
    shifted = jax.vmap(
        lambda rows, shift_by: lax.dynamic_slice_in_dim(rows, total_len - shift_by, total_len, 2),
        in_axes=(2, 0),
        out_axes=2,
    )(doubled, station_delays)
    own_weights = lax.dynamic_slice_in_dim(
        beam_weights, lax.axis_index("sta") * local_beams, local_beams, 2
    )
    shard_piece = lax.all_gather(shifted, "sta", axis=2, tiled=True)
    beams = beam_terms(own_weights, shard_piece[:, 0], shard_piece[:, 1])
    cos_root, sin_root = angle_tables(root_len, root_len)
    cos_twist, sin_twist = angle_tables(root_len, total_len)
    x_real = beams[:, :, 0].reshape(local_beams, sub_dev, root_len, root_len)
    x_imag = beams[:, :, 1].reshape(local_beams, sub_dev, root_len, root_len)
    a_real, a_imag = left_dft(cos_root, sin_root, x_real, x_imag, 1.0)
    b_real = a_real * cos_twist + a_imag * sin_twist
    b_imag = a_imag * cos_twist - a_real * sin_twist
    s_real, s_imag = right_dft(cos_root, sin_root, b_real, b_imag, 1.0)
    subband = lax.axis_index("sub") * sub_dev + jnp.arange(sub_dev, dtype=jnp.int32)
    base_phase = chirp_base(subband, root_len, total_len)
    dm_value = DM_STEP * dm_index.astype(jnp.float32)
    phase_table = dm_value[:, None, :, None, None] * base_phase[None, :, None, :, :]
    h_real = jnp.cos(phase_table)
    h_imag = jnp.sin(phase_table)
    c_real = s_real[:, :, None] * h_real - s_imag[:, :, None] * h_imag
    c_imag = s_real[:, :, None] * h_imag + s_imag[:, :, None] * h_real
    d_real, d_imag = right_dft(cos_root, sin_root, c_real, c_imag, -1.0)
    e_real = d_real * cos_twist - d_imag * sin_twist
    e_imag = d_imag * cos_twist + d_real * sin_twist
    scale = 1.0 / total_len
    out_real = jnp.einsum("tk,bsjku->sbjtu", cos_root, e_real, precision=HIGHEST) - jnp.einsum(
        "tk,bsjku->sbjtu", sin_root, e_imag, precision=HIGHEST
    )
    out_imag = jnp.einsum("tk,bsjku->sbjtu", cos_root, e_imag, precision=HIGHEST) + jnp.einsum(
        "tk,bsjku->sbjtu", sin_root, e_real, precision=HIGHEST
    )
    series = jnp.stack([out_real * scale, out_imag * scale], axis=1).reshape(
        sub_dev, 2, local_beams, trials, total_len
    )
    n_sub = lax.axis_size("sub")
    n_sta = lax.axis_size("sta")
    moved = lax.all_to_all(series[None], ("sub", "sta"), split_axis=5, concat_axis=0, tiled=True)
    moved = moved.reshape(n_sub, n_sta, sub_dev, 2, local_beams, trials, -1)
    moved = moved.transpose(0, 2, 3, 1, 4, 5, 6).reshape(
        n_sub * sub_dev, 2, n_sta * local_beams, trials, -1
    )
    intensity = jnp.mean(moved[:, 0] * moved[:, 0] + moved[:, 1] * moved[:, 1], axis=0)
    return (moved, intensity)


def solution(mesh):
    return jax.shard_map(
        shards,
        mesh=mesh,
        in_specs=(
            P("sub", None, "sta", None),
            P("sub", None, None, None),
            P("sta"),
            P("sta", None),
        ),
        out_specs=(P(None, None, None, None, ("sub", "sta")), P(None, None, ("sub", "sta"))),
        check_vma=False,
    )
```

profile of v0, /device:TPU:0, one launch (start us, length us, event | category | flops | bytes accessed | tf_op | source)
XLA Modules:
  0.0 1215.7 jit_solution(15129982250046369785)
XLA Ops:
  7.9 6.5 copy.86
  14.4 9.1 maximum_bitcast_fusion
  23.6 62.1 %while.1 = (s32[]{:T(128)}, bf16[16,1,2,131072]{3,2,1,0:T(2,128)(2,1)}, s32[16,4]{0,1:T(4,128)S(1)}, bf16[16,1,2,65536]{3,2,1,0:T(2,128)(2,1)}, s32[]{:T(128)}) while((s32[]{:T(128)}, bf16[16,1,2,131072]{3,2,1,0:T(2,128)(2,1)}, s32[16,4]{0,1:T(4,128)S(1)}, bf16[16,1,2,65536]{3,2,1,0:T(2,128)(2,1)}, s32[]{:T(128)}) %tuple.27), condition=%wide.while_cond, body=%wide.while_body.sunk | while | flops 2 | bytes 525437 | solution.py:73
  85.7 6.4 copy.122
  93.6 158.7 %all-gather.2.cloned.1.call-done = bf16[1,2,64,65536]{3,2,1,0:T(8,128)(2,1)} async-done(((bf16[1,2,16,65536]{3,2,1,0:T(8,128)(2,1)}), bf16[1,2,64,65536]{3,2,1,0:T(8,128)(2,1)}) %all-gather.2.cloned.1.call-update) | async-done | bytes 16777232 | tf_op jit(solution)/shard_map/all_gather | solution.py:80
  256.9 6.1 convolution_add_fusion
  274.1 6.1 convolution_subtract_fusion
  293.7 4.9 fusion.25
  307.7 5.1 fusion.17
  312.8 10.3 fusion.44
  323.1 10.2 fusion.46
  333.3 10.4 multiply_subtract_fusion.1
  343.7 10.6 multiply_add_fusion.1
  359.1 5.7 fusion.23
  364.8 5.8 multiply_bitcast_fusion
  377.1 7.9 multiply_bitcast_fusion.1
  393.1 114.7 %copy.105 = f32[1,1,2,8,1,65536]{3,4,2,1,0,5:T(1,128)} copy(f32[1,1,2,8,1,65536]{5,3,4,2,1,0:T(8,128)} %pad_maximum_fusion) | data formatting | bytes 8388608 | tf_op jit(solution)/shard_map/stack | solution.py:108
  508.3 240.9 %reduce.2 = f32[65536,2,8]{2,1,0:T(2,128)} reduce(f32[65536,1,1,2,1,8]{5,4,3,2,1,0:T(1,128)} %bitcast.142, f32[]{:T(128)} %broadcast.336), dimensions={1,2,4}, to_apply=%bitcast.142.reduce_sub_computation | reduce | bytes 8388612
  749.2 109.1 %reshape.375 = f32[32,1,32768]{2,1,0:T(1,128)} reshape(f32[65536,2,8]{2,1,0:T(2,128)} %reduce.2) | data formatting | bytes 8388608
  858.3 99.1 %all_to_all.15 = f32[32,1,32768]{2,1,0:T(1,128)} all-to-all(f32[32,1,32768]{2,1,0:T(1,128)} %reshape.375), channel_id=1, replica_groups=mesh['sub'=8,'sta'=4] {'sub','sta'}, dimensions={0} | all-to-all | bytes 8388608 | tf_op jit(solution)/shard_map/all_to_all | solution.py:113
  957.5 13.8 %reduce.3 = f32[32,32768]{1,0:T(8,128)} reduce(f32[32,1,32768]{2,1,0:T(1,128)} %all_to_all.15, f32[]{:T(128)} %broadcast.336), dimensions={1}, to_apply=%all_to_all.11.reduce_sub_computation | reduce | bytes 8388612 | tf_op jit(solution)/shard_map/all_to_all | solution.py:113
  971.2 171.1 %reshape.376 = f32[65536,1,1,2,1,8]{5,4,3,2,1,0:T(1,128)} reshape(f32[32,32768]{1,0:T(8,128)} %reduce.3) | data formatting | bytes 8388608
  1142.3 53.6 %copy.118 = f32[1,1,2,8,1,32,2048]{6,5,3,2,4,1,0:T(8,128)} copy(f32[1,1,2,8,1,32,2048]{3,2,6,5,4,1,0:T(2,128)} %bitcast.32) | data formatting | bytes 8388608 | tf_op jit(solution)/shard_map/all_to_all | solution.py:113
  1201.3 6.4 copy.109
  (94 shorter events, 128.6 us)
Async XLA Ops:
  7.2 245.1 %copy-start = (bf16[1,2,32,64]{3,2,1,0:T(8,128)(2,1)S(1)}, bf16[1,2,32,64]{3,2,1,0:T(8,128)(2,1)}, u32[]{:S(2)}) copy-start(bf16[1,2,32,64]{3,2,1,0:T(8,128)(2,1)} %param.5) | copy-start | bytes 24580
  7.2 245.1 %all-gather.2.cloned.1.call-start = ((), (), s32[]{:S(2)}) async-start(), calls=%async_computation.1 | async-start | bytes 20971520 | tf_op jit(solution)/shard_map/all_gather | solution.py:80
  92.1 1.4 copy-start.5
  283.2 4.6 copy-start.3
  283.2 4.6 copy-start.4
  354.4 10.5 copy-start.2
  1201.3 7.3 copy-start.1
Sparse Core Ops, SparseCore 0:
  92.2 160.0 all-gather.1
where the time goes:
time: 1230 us; the launch traced here: 1220 us
  local copies, waits for them, and re-layouts  552 us (45%)
  other arithmetic  271 us (22%)
  waiting for transfers between devices  159 us (13%)
  matrix products  121 us (10%)
  blocking collectives  99.1 us (8%)
  between operations  14.6 us (1%)
    unnamed x18, local copies, waits for them, and re-layouts  294 us
    unnamed x2, other arithmetic  241 us
    all_gather x1, waiting for transfers between devices, shards(): shard_piece = lax.all_gather(shifted, 'sta', axis=2, tiled=True)  159 us
    another operation x3, local copies, waits for them, and re-layouts, shards(): jnp.stack([out_real * scale, out_imag * scale], axis=1)  120 us
    all_to_all x1, blocking collectives, shards(): lax.all_to_all(series[None], ('sub', 'sta'), split_axis=5, concat_axis=0,...  99.1 us
    gather x48, local copies, waits for them, and re-layouts  62.1 us
    all_to_all x2, local copies, waits for them, and re-layouts, shards(): lax.all_to_all(series[None], ('sub', 'sta'), split_axis=5, concat_axis=0,...  58.2 us
  transfers between devices with their start and end apart: 1, of which 1 were waited for; matrix products, arithmetic and copies ran while one was open for 0% of the time, Pallas kernels for 0%

commit v1 on v0

--- a/solution.py
+++ b/solution.py
@@ -10,6 +10,19 @@
 BASE_FREQ = 120.0
 CHANNEL_WIDTH = 0.1953125
 HIGHEST = lax.Precision.HIGHEST
+
+
+def desk_begin(join_dim, chip_axis, dim_k, arr):
+    mid_arr = jnp.concatenate(
+        jax.lax.all_to_all(
+            jnp.stack(jnp.split(arr, jax.lax.axis_size(chip_axis), axis=join_dim), axis=0),
+            chip_axis,
+            0,
+            0,
+        ),
+        dim_k,
+    )
+    return mid_arr
 
 
 def angle_tables(rows_len, modulus):
@@ -110,7 +123,7 @@
     )
     n_sub = lax.axis_size("sub")
     n_sta = lax.axis_size("sta")
-    moved = lax.all_to_all(series[None], ("sub", "sta"), split_axis=5, concat_axis=0, tiled=True)
+    moved = desk_begin(5, ("sub", "sta"), 0, series[None])
     moved = moved.reshape(n_sub, n_sta, sub_dev, 2, local_beams, trials, -1)
     moved = moved.transpose(0, 2, 3, 1, 4, 5, 6).reshape(
         n_sub * sub_dev, 2, n_sta * local_beams, trials, -1

time: 1230 us -> 511 us (0.42)
  local copies, waits for them, and re-layouts: 552 us -> 102 us
  other arithmetic: 271 us -> 10.8 us
    unnamed x18 -> x51, local copies, waits for them, and re-layouts: 294 us -> 15.5 us
    unnamed x2 -> x1, other arithmetic: 241 us -> 0.01 us
    another operation x3, local copies, waits for them, and re-layouts: 120 us -> 5.12 us  [shards(): jnp.stack([out_real * scale, out_imag * scale], axis=1)]
    all_to_all x2 -> x0, local copies, waits for them, and re-layouts: 58.2 us -> none  [shards(): lax.all_to_all(series[None], ('sub', 'sta'), split_axis=5, concat_axis=0,...]
    all_to_all x1 -> x0, other arithmetic: 13.8 us -> none  [shards(): lax.all_to_all(series[None], ('sub', 'sta'), split_axis=5, concat_axis=0,...]
where the time goes in v1:
time: 511 us; the launch traced here: 506 us
  waiting for transfers between devices  159 us (31%)
  matrix products  121 us (24%)
  local copies, waits for them, and re-layouts  102 us (20%)
  blocking collectives  98.7 us (19%)
  between operations  14.9 us (3%)
  other arithmetic  10.8 us (2%)
    all_gather x1, waiting for transfers between devices, shards(): shard_piece = lax.all_gather(shifted, 'sta', axis=2, tiled=True)  159 us
    all_to_all x1, blocking collectives, desk_begin(): jax.lax.all_to_all(jnp.stack(jnp.split(arr, jax.lax.axis_size(chip_axis),...  98.7 us
    gather x48, local copies, waits for them, and re-layouts  62.9 us
    unnamed x51, local copies, waits for them, and re-layouts  15.5 us
    dot_general x2, matrix products, right_dft(): jnp.einsum('...kt,tm->...km', x_real, sin_table, precision=HIGHEST)  15.5 us
    dot_general x2, matrix products, right_dft(): jnp.einsum('...kt,tm->...km', x_imag, sin_table, precision=HIGHEST)  15.4 us
    dot_general x2, matrix products, right_dft(): jnp.einsum('...kt,tm->...km', x_real, cos_table, precision=HIGHEST)  14.9 us
    dot_general x2, matrix products, right_dft(): jnp.einsum('...kt,tm->...km', x_imag, cos_table, precision=HIGHEST)  14.8 us
  transfers between devices with their start and end apart: 1, of which 1 were waited for; matrix products, arithmetic and copies ran while one was open for 0% of the time, Pallas kernels for 0%

profile of v1, /device:TPU:0, one launch (start us, length us, event | category | flops | bytes accessed | tf_op | source)
XLA Modules:
  0.0 505.7 jit_solution(10406041938670500814)
XLA Ops:
  7.2 6.5 %copy.72 = bf16[1,2,16,65536]{3,1,0,2:T(2,128)(2,1)S(1)} copy(bf16[1,2,16,65536]{3,2,1,0:T(8,128)(2,1)} %param.4) | data formatting | bytes 8388608 | tf_op args[0]
  13.8 9.2 %maximum_bitcast_fusion = bf16[16,1,2,131072]{3,2,1,0:T(2,128)(2,1)} fusion(bf16[1,2,16,65536]{3,1,0,2:T(2,128)(2,1)S(1)} %copy.72), kind=kLoop, calls=%fused_computation.6 | loop fusion | flops 16777216 | bytes 12582912 | tf_op jit(solution)/shard_map/vmap()/transpose | solution.py:86
  23.0 62.9 %while.1 = (s32[]{:T(128)}, bf16[16,1,2,131072]{3,2,1,0:T(2,128)(2,1)}, s32[16,4]{0,1:T(4,128)S(1)}, bf16[16,1,2,65536]{3,2,1,0:T(2,128)(2,1)}, s32[]{:T(128)}) while((s32[]{:T(128)}, bf16[16,1,2,131072]{3,2,1,0:T(2,128)(2,1)}, s32[16,4]{0,1:T(4,128)S(1)}, bf16[16,1,2,65536]{3,2,1,0:T(2,128)(2,1)}, s32[]{:T(128)}) %tuple.25), condition=%wide.while_cond, body=%wide.while_body.sunk | while | flops 2 | bytes 525937 | solution.py:86
  85.9 6.4 %copy.135 = bf16[16,1,2,65536]{3,0,2,1:T(8,128)(2,1)} copy(bf16[16,1,2,65536]{3,2,1,0:T(2,128)(2,1)} %get-tuple-element.9) | data formatting | bytes 8388608 | tf_op jit(solution)/shard_map/vmap()/gather | solution.py:86
  93.9 158.7 %all-gather.2.cloned.1.call-done = bf16[1,2,64,65536]{3,2,1,0:T(8,128)(2,1)} async-done(((bf16[1,2,16,65536]{3,2,1,0:T(8,128)(2,1)}), bf16[1,2,64,65536]{3,2,1,0:T(8,128)(2,1)}) %all-gather.2.cloned.1.call-update) | async-done | bytes 16777232 | tf_op jit(solution)/shard_map/all_gather | solution.py:93
  252.6 4.6 fusion.1
  257.1 6.1 %convolution_add_fusion = f32[65536,8]{0,1:T(8,128)} fusion(f32[65536,8]{0,1:T(8,128)S(1)} %fusion.1, bf16[1,2,64,65536]{3,2,1,0:T(8,128)(2,1)} %all-gather.2.cloned.1.call-done, bf16[1,2,32,64]{3,2,1,0:T(8,128)(2,1)S(1)} %copy-done, s32[]{:T(128)S(6)} %add.214, s32[]{:T(128)S(6)} %select_n.87), kind=kOutput, calls=%fused_computation.2 | convolution fusion | flops 67633152 | bytes 12584968 | tf_op jit(solution)/shard_map/sbk,skt->bst/dot_general | solution.py:74
  269.8 4.6 fusion
  274.4 6.1 %convolution_subtract_fusion = f32[65536,8]{0,1:T(8,128)} fusion(f32[65536,8]{0,1:T(8,128)S(1)} %fusion, bf16[1,2,64,65536]{3,2,1,0:T(8,128)(2,1)} %all-gather.2.cloned.1.call-done, bf16[1,2,32,64]{3,2,1,0:T(8,128)(2,1)S(1)} %copy-done, s32[]{:T(128)S(6)} %add.214, s32[]{:T(128)S(6)} %select_n.87), kind=kOutput, calls=%fused_computation.3 | convolution fusion | flops 67633152 | bytes 12584968 | tf_op jit(solution)/shard_map/sbk,skt->bst/dot_general | solution.py:71
  283.6 4.6 fusion.52
  294.0 4.9 fusion.25
  298.9 4.6 fusion.27
  303.5 4.6 fusion.20
  308.1 5.1 %fusion.17 = f32[8,256,256]{2,1,0:T(8,128)S(1)} fusion(f32[8,256,256]{2,1,0:T(8,128)S(1)} %fusion.27, f32[8,256,256]{2,1,0:T(8,128)S(1)} %convolution_add_fusion.1, f32[8,256,256]{2,1,0:T(8,128)S(1)} %convolution_subtract_fusion.1, f32[256,256]{0,1:T(8,128)S(1)} %copy.80, f32[256,256]{0,1:T(8,128)S(1)} %copy.77), kind=kOutput, calls=%fused_computation.40 | convolution fusion | flops 1613627392 | bytes 8912896 | tf_op jit(solution)/shard_map/...kt,tm->...km/dot_general | solution.py:59
  313.2 10.3 %fusion.46 = f32[8,256,256]{2,1,0:T(8,128)S(1)} fusion(f32[8,256,256]{2,1,0:T(8,128)S(1)} %fusion.20, f32[8,256,256]{2,1,0:T(8,128)S(1)} %fusion.17, f32[256,256]{1,0:T(8,128)S(1)} %multiply_divide_fusion, f32[8]{0:T(128)S(1)} %multiply_bitcast_fusion.2), kind=kOutput, calls=%fused_computation.71 | convolution fusion | flops 1613627392 | bytes 6553632 | tf_op jit(solution)/shard_map/...kt,tm->...km/dot_general | solution.py:57
  323.5 10.1 %fusion.44 = f32[8,256,256]{2,1,0:T(8,128)S(1)} fusion(f32[8,256,256]{2,1,0:T(8,128)S(1)} %fusion.17, f32[8,256,256]{2,1,0:T(8,128)S(1)} %fusion.20, f32[256,256]{1,0:T(8,128)S(1)} %multiply_divide_fusion, f32[8]{0:T(128)S(1)} %multiply_bitcast_fusion.2), kind=kOutput, calls=%fused_computation.69 | convolution fusion | flops 1613627392 | bytes 6553632 | tf_op jit(solution)/shard_map/...kt,tm->...km/dot_general | solution.py:60
  333.7 10.4 %multiply_add_fusion.1 = f32[8,256,256]{2,1,0:T(8,128)S(1)} fusion(f32[8,256,256]{2,1,0:T(8,128)S(1)} %fusion.46, f32[8,256,256]{2,1,0:T(8,128)S(1)} %fusion.17, f32[8,256,256]{2,1,0:T(8,128)S(1)} %fusion.20, f32[256,256]{1,0:T(8,128)S(1)} %multiply_divide_fusion, f32[8]{0:T(128)S(1)} %multiply_bitcast_fusion.2), kind=kOutput, calls=%fused_computation.39 | convolution fusion | flops 1614675968 | bytes 8650784 | tf_op jit(solution)/shard_map/...kt,tm->...km/dot_general | solution.py:59
  344.0 10.6 %multiply_subtract_fusion.1 = f32[8,256,256]{2,1,0:T(8,128)S(1)} fusion(f32[8,256,256]{2,1,0:T(8,128)S(1)} %fusion.44, f32[8,256,256]{2,1,0:T(8,128)S(1)} %fusion.20, f32[8,256,256]{2,1,0:T(8,128)S(1)} %fusion.17, f32[256,256]{1,0:T(8,128)S(1)} %multiply_divide_fusion, f32[8]{0:T(128)S(1)} %multiply_bitcast_fusion.2), kind=kOutput, calls=%fused_computation.38 | convolution fusion | flops 1614675968 | bytes 8650784 | tf_op jit(solution)/shard_map/...kt,tm->...km/dot_general | solution.py:62
  354.6 4.7 fusion.24
  359.4 5.7 %fusion.23 = f32[8,256,256]{2,1,0:T(8,128)} fusion(f32[8,256,256]{2,1,0:T(8,128)S(1)} %multiply_subtract_fusion.1, f32[8,256,256]{2,1,0:T(8,128)S(1)} %multiply_add_fusion.1, f32[256,256]{1,0:T(8,128)S(1)} %get-tuple-element.22, f32[256,256]{1,0:T(8,128)S(1)} %get-tuple-element.23), kind=kOutput, calls=%fused_computation.45 | convolution fusion | flops 1613103104 | bytes 6815744 | tf_op jit(solution)/shard_map/tk,bsjku->sbjtu/dot_general | solution.py:115
  365.1 5.8 %multiply_bitcast_fusion = f32[1,8,1,256,256]{3,4,1,2,0:T(8,128)} fusion(f32[8,256,256]{2,1,0:T(8,128)S(1)} %fusion.24, f32[8,256,256]{2,1,0:T(8,128)S(1)} %multiply_subtract_fusion.1, f32[8,256,256]{2,1,0:T(8,128)S(1)} %multiply_add_fusion.1, f32[256,256]{1,0:T(8,128)S(1)} %get-tuple-element.22, f32[256,256]{1,0:T(8,128)S(1)} %get-tuple-element.23), kind=kOutput, calls=%fused_computation.34 | convolution fusion | flops 1614151680 | bytes 8912896 | tf_op jit(solution)/shard_map/tk,bsjku->sbjtu/dot_general | solution.py:118
  377.3 7.9 %multiply_bitcast_fusion.1 = f32[1,8,1,256,256]{3,4,1,2,0:T(8,128)} fusion(f32[8,256,256]{2,1,0:T(8,128)} %fusion.23, f32[8,256,256]{2,1,0:T(8,128)S(1)} %multiply_add_fusion.1, f32[8,256,256]{2,1,0:T(8,128)} %copy-done.2, f32[256,256]{1,0:T(8,128)S(1)} %get-tuple-element.22, f32[256,256]{1,0:T(8,128)S(1)} %get-tuple-element.23), kind=kOutput, calls=%fused_computation.35 | convolution fusion | flops 1614151680 | bytes 8912896 | tf_op jit(solution)/shard_map/tk,bsjku->sbjtu/dot_general | solution.py:115
  391.9 98.7 %all_to_all.5 = f32[32,1,1,2,8,1,2048]{6,4,3,5,2,1,0:T(8,128)S(1)} all-to-all(f32[32,1,1,2,8,1,2048]{6,4,3,5,2,1,0:T(8,128)S(1)} %fusion.63), channel_id=1, replica_groups=mesh['sub'=8,'sta'=4] {'sub','sta'}, dimensions={0} | all-to-all | bytes 8388608 | tf_op jit(solution)/shard_map/all_to_all | solution.py:17
  490.8 6.4 %copy.123 = f32[8,2,32,1,2048]{4,3,2,1,0:T(1,128)} copy(f32[8,2,32,1,2048]{4,2,1,0,3:T(8,128)S(1)} %bitcast.309) | data formatting | bytes 8388608
  (123 shorter events, 94.3 us)
Async XLA Ops:
  7.2 245.4 %copy-start = (bf16[1,2,32,64]{3,2,1,0:T(8,128)(2,1)S(1)}, bf16[1,2,32,64]{3,2,1,0:T(8,128)(2,1)}, u32[]{:S(2)}) copy-start(bf16[1,2,32,64]{3,2,1,0:T(8,128)(2,1)} %param.5) | copy-start | bytes 24580
  7.2 245.4 %all-gather.2.cloned.1.call-start = ((), (), s32[]{:S(2)}) async-start(), calls=%async_computation.1 | async-start | bytes 20971520 | tf_op jit(solution)/shard_map/all_gather | solution.py:93
  13.7 9.2 %copy-start.6 = (s32[16]{0:T(128)S(1)}, s32[16]{0:T(128)}, u32[]{:S(2)}) copy-start(s32[16]{0:T(128)} %param.6) | copy-start | bytes 196
  92.4 1.4 copy-start.7
  283.6 4.6 copy-start.3
  283.6 4.6 copy-start.4
  354.6 10.5 %copy-start.2 = (f32[8,256,256]{2,1,0:T(8,128)}, f32[8,256,256]{2,1,0:T(8,128)S(1)}, u32[]{:S(2)}) copy-start(f32[8,256,256]{2,1,0:T(8,128)S(1)} %multiply_subtract_fusion.1) | copy-start | bytes 6291460
  388.9 2.2 copy-start.5
  490.8 7.7 %copy-start.1 = (bf16[1,2,32,64]{3,2,1,0:T(8,128)(2,1)S(1)}, bf16[1,2,32,64]{3,2,1,0:T(8,128)(2,1)}, u32[]{:S(2)}) copy-start(bf16[1,2,32,64]{3,2,1,0:T(8,128)(2,1)} %param.5) | copy-start | bytes 24580
Sparse Core Ops, SparseCore 0:
  92.5 160.0 all-gather.1
